TPU v7x, 256 devices: a whole 4x4x8 slice. The times are simulated.
256 devices in a mesh: shard: 64 (over z, y, core), model: 4 (over x).
Axes of the slice: x: 4, y: 4, z: 8, core: 2. Of those that a mesh axis runs over, the one named last changes fastest.
Arguments:
- one_gate: float32 [2048, 8192], P('shard', 'model'), may hold values from -0.375 to 0.375
- other_gate: float32 [2048, 8192], P('shard', 'model'), may hold values from -0.125 to 0.125
- one_up: float32 [2048, 8192], P('shard', 'model'), may hold values from -0.375 to 0.375
- other_up: float32 [2048, 8192], P('shard', 'model'), may hold values from -0.125 to 0.125
- mix_share: float32 [2048], P('shard'), may hold values from 0.2 to 0.8
- norm_train: float32 [2048], P(('shard', 'model')), may hold values from 0.25 to 1.75
- norm_step: float32 [2048], P(('shard', 'model')), may hold values from -0.3 to 0.3
Outputs:
- final_gate: bfloat16 [2048, 8192], P(None, 'model')
- final_up: bfloat16 [2048, 8192], P(None, 'model')
- column_gate: float32 [8192], P('model')
- column_up: float32 [8192], P('model')
- serve_norm: bfloat16 [2048], replicated
All inputs are finite; a program needn't handle non-finite values. Where the computation divides by a largest or mean magnitude, that divisor is 1e-20 or more.
Results may differ from a plain program's by a relative error of at most 0.001.
Values may be sent and summed in bfloat16 or wider, within the bound.
No kernel may reach another device: no remote copies, remote signals or barrier semaphores. Data moves between devices by JAX's collectives and lax.ppermute only.
A program may use at most 128 MiB of HBM per device.

v0:
```python
import jax
import jax.numpy as jnp
from jax import lax
from jax.sharding import Mesh
from jax.sharding import PartitionSpec as P

SHARD = ("shard_0", "shard_1", "shard_2")
SHARD_MODEL = ("shard_0", "shard_1", "shard_2", "model")


def copy_for_each(array, axis):
    copies = jnp.broadcast_to(array, (lax.axis_size(axis), *array.shape))
    return lax.all_to_all(copies, axis, split_axis=0, concat_axis=0, tiled=True)


def over_copies(array, axis):
    return copy_for_each(array, axis).max(axis=0)


def in_one(arrays, axis):
    flat, at, outs = (jnp.concatenate([a.reshape(-1) for a in arrays]), 0, [])
    total = over_copies(flat, axis)
    for a in arrays:
        outs.append(total[at : at + a.size].reshape(a.shape))
        at += a.size
    return tuple(outs)


def side_by_side(arrays, axis, dim, along):
    both = jnp.concatenate(arrays, axis=along)
    whole, at, outs = (lax.all_gather(both, axis, axis=dim, tiled=True), 0, [])
    for a in arrays:
        outs.append(lax.slice_in_dim(whole, at, at + a.shape[along], axis=along))
        at += a.shape[along]
    return tuple(outs)


def joined_along(tiles, dim):
    dims = list(tiles.shape[1:])
    dims[dim] *= tiles.shape[0]
    return jnp.moveaxis(tiles, 0, dim).reshape(dims)


def gather_in_order(array, axes, turns):
    tiles = array[None]
    for k in turns:
        tiles = lax.all_gather(tiles, axes[k], axis=0, tiled=True)
    carried = [lax.axis_size(axes[k]) for k in reversed(turns)]
    tiles = tiles.reshape(*carried, *array.shape)
    turned = sorted(range(len(turns)), key=lambda place: turns[len(turns) - 1 - place])
    return tiles.transpose(*turned, *range(len(turns), tiles.ndim)).reshape(-1, *array.shape)


def gathered_by_axis(array, axes, turns, dim):
    return joined_along(gather_in_order(array, axes, turns), dim)


def local(one_gate, other_gate, one_up, other_up, mix_share, norm_train, norm_step):
    result_gate = mix_share[:, None] * one_gate + (1.0 - mix_share[:, None]) * other_gate
    result_up = mix_share[:, None] * one_up + (1.0 - mix_share[:, None]) * other_up
    column_gate, column_up = in_one(
        (jnp.max(jnp.abs(result_gate), axis=0), jnp.max(jnp.abs(result_up), axis=0)), SHARD
    )
    narrow_gate, narrow_up = (
        (result_gate / column_gate).astype(jnp.bfloat16),
        (result_up / column_up).astype(jnp.bfloat16),
    )
    final_gate, final_up = side_by_side((narrow_gate, narrow_up), SHARD, 0, 1)
    serve_norm = gathered_by_axis(
        (norm_train + norm_step).astype(jnp.bfloat16), SHARD_MODEL, (0, 1, 3, 2), 0
    )
    return (final_gate, final_up, column_gate, column_up, serve_norm)


def solution(mesh):
    torus = Mesh(
        mesh.devices.reshape(8, 4, 2, mesh.shape["model"]),
        ("shard_0", "shard_1", "shard_2", "model"),
    )
    return jax.shard_map(
        local,
        mesh=torus,
        in_specs=(
            P(SHARD, "model"),
            P(SHARD, "model"),
            P(SHARD, "model"),
            P(SHARD, "model"),
            P(SHARD),
            P(SHARD_MODEL),
            P(SHARD_MODEL),
        ),
        out_specs=(P(None, "model"), P(None, "model"), P("model"), P("model"), P()),
        check_vma=False,
    )
```

profile of v0, /device:TPU:1, one launch (start us, length us, event | category | flops | bytes accessed | tf_op | source)
XLA Modules:
  0.0 169.9 jit_solution(2794008969568539526)
XLA Ops:
  7.2 0.0 all-gather.4.cloned.1.call-start
  7.2 0.7 broadcast_subtract_fusion
  7.9 1.4 abs_reduce_fusion.1
  9.3 1.0 broadcast_in_dim.4
  10.3 41.1 %all_to_all.6 = f32[64,1,4096]{2,1,0:T(1,128)S(1)} all-to-all(f32[64,1,4096]{2,1,0:T(1,128)S(1)} %broadcast_in_dim.4), channel_id=1, replica_groups=mesh['shard_0'=8,'shard_1'=4,'shard_2'=2,'model'=4] {'shard_0','shard_1'..., dimensions={0} | all-to-all | bytes 2097152 | tf_op jit(solution)/shard_map/all_to_all | solution.py:13
  51.4 0.9 reduce_max.29
  52.3 1.4 divide_convert_fusion.1
  53.6 0.7 pad_maximum_fusion
  54.4 0.0 all-gather.4.cloned.1.call-update
  54.4 1.3 dynamic-slice
  56.3 0.7 add_convert_fusion
  57.0 0.2 dynamic-update-slice
  57.2 12.8 %all-reduce = bf16[64]{0:T(256)(128)(2,1)S(1)} all-reduce(bf16[64]{0:T(256)(128)(2,1)S(1)} %dynamic-update-slice), channel_id=2, replica_groups=mesh['shard_0'=8,'shard_1'=4,'shard_2'=2,'model'=4] {'shard_0'}, use_global_device_ids=true, to_apply=%add | all-reduce | flops 64 | bytes 256
  70.0 0.1 reshape.23
  70.1 8.9 %all_gather.17 = bf16[32,8]{1,0:T(8,128)(2,1)S(1)} all-gather(bf16[8,8]{1,0:T(8,128)(2,1)S(1)} %reshape.23), channel_id=1, replica_groups=mesh['shard_0'=8,'shard_1'=4,'shard_2'=2,'model'=4] {'shard_1'}, dimensions={0}, use_global_device_ids=true | all-gather | bytes 640 | tf_op jit(solution)/shard_map/all_gather | solution.py:47
  79.0 0.1 copy.23
  79.1 8.9 %all-gather.1 = bf16[4,32,8]{1,2,0:T(8,128)(2,1)S(1)} all-gather(bf16[1,32,8]{1,2,0:T(8,128)(2,1)S(1)} %copy.23), channel_id=1, replica_groups=mesh['shard_0'=8,'shard_1'=4,'shard_2'=2,'model'=4] {'model'}, dimensions={0}, use_global_device_ids=true | all-gather | bytes 2560 | tf_op jit(solution)/shard_map/all_gather | solution.py:47
  88.0 0.1 reshape.28
  88.1 9.0 %all_gather.19 = bf16[256,8]{0,1:T(8,128)(2,1)S(1)} all-gather(bf16[128,8]{0,1:T(8,128)(2,1)S(1)} %reshape.28), channel_id=1, replica_groups=mesh['shard_0'=8,'shard_1'=4,'shard_2'=2,'model'=4] {'shard_2'}, dimensions={0}, use_global_device_ids=true | all-gather | bytes 6144 | tf_op jit(solution)/shard_map/all_gather | solution.py:47
  97.1 0.1 reshape.22
  97.3 0.2 copy.25
  97.5 0.7 reshape_reshape.3
  98.2 53.0 %all-gather.4.cloned.1.call-done = bf16[2048,4096]{1,0:T(8,128)(2,1)} async-done(((bf16[32,4096]{1,0:T(8,128)(2,1)}), bf16[2048,4096]{1,0:T(8,128)(2,1)}) %all-gather.4.cloned.1.call-update) | async-done | bytes 16777232 | tf_op jit(solution)/shard_map/all_gather | solution.py:31
  151.1 11.9 %fusion = (bf16[2048,2048]{1,0:T(8,128)(2,1)}, bf16[2048,2048]{1,0:T(8,128)(2,1)}) fusion(bf16[2048,4096]{1,0:T(8,128)(2,1)} %all-gather.4.cloned.1.call-done), kind=kLoop, calls=%fused_computation.10 | loop fusion | bytes 33554432 | tf_op jit(solution)/shard_map/slice | solution.py:33
  (8 shorter events, 0.0 us)
Async XLA Ops:
  7.2 144.0 %all-gather.4.cloned.1.call-start = ((), (), s32[]{:S(2)}) async-start(), calls=%async_computation.1 | async-start | bytes 17039360 | tf_op jit(solution)/shard_map/all_gather | solution.py:31
  52.3 110.8 %copy-start = (f32[2048]{0:T(1024)}, f32[2048]{0:T(1024)S(1)}, u32[]{:S(2)}) copy-start(f32[2048]{0:T(1024)S(1)} %get-tuple-element.9) | copy-start | bytes 24580
  52.3 110.8 %copy-start.1 = (f32[2048]{0:T(1024)}, f32[2048]{0:T(1024)S(1)}, u32[]{:S(2)}) copy-start(f32[2048]{0:T(1024)S(1)} %get-tuple-element.10) | copy-start | bytes 24580
Sparse Core Ops, SparseCore 0:
  54.5 96.5 all-gather.3
where the time goes:
time: 170 us
  blocking collectives  80.8 us (48%)
  waiting for transfers between devices  53 us (31%)
  local copies, waits for them, and re-layouts  15.7 us (9%)
  between operations  14.8 us (9%)
  other arithmetic  5.66 us (3%)
    all_gather x1, waiting for transfers between devices, side_by_side(): whole, at, outs = (lax.all_gather(both, axis, axis=dim, tiled=True), 0, [])  53 us
    all_to_all x1, blocking collectives, copy_for_each(): return lax.all_to_all(copies, axis, split_axis=0, concat_axis=0, tiled=True)  41.1 us
    all_gather x3, blocking collectives, gather_in_order(): tiles = lax.all_gather(tiles, axes[k], axis=0, tiled=True)  26.8 us
    unnamed x1, blocking collectives  12.8 us
    slice x1, local copies, waits for them, and re-layouts, side_by_side(): outs.append(lax.slice_in_dim(whole, at, at + a.shape[along], axis=along))  11.9 us
  transfers between devices with their start and end apart: 1, of which 1 were waited for; matrix products, arithmetic and copies ran while one was open for 2% of the time, Pallas kernels for 0%

commit v1 on v0

v1 whole, which is shorter than its diff:
```python
import jax
import jax.numpy as jnp
from jax import lax
from jax.experimental import pallas as pl
from jax.experimental.pallas import tpu as pltpu
from jax.sharding import Mesh
from jax.sharding import PartitionSpec as P


SHARD = ("z", "y", "core")
ALL = ("z", "y", "core", "model")
Z, Y, C, X = 8, 4, 2, 4
ROWS = 64
W = 2048
A = 1536


def pairs(target):
    at = lambda z, y, c: ((z % Z) * Y + y % Y) * C + c
    return [
        (at(z, y, c), at(*target(z, y, c)))
        for z in range(Z)
        for y in range(Y)
        for c in range(C)
    ]


def way(c):
    return 1 - 2 * c


def along_z(v, k=1):
    return lax.ppermute(v, SHARD, pairs(lambda z, y, c: (z + k * way(c), y, c)))


def along_y(v, k=1):
    return lax.ppermute(v, SHARD, pairs(lambda z, y, c: (z, y + k * way(c), c)))


def swap(v):
    return lax.ppermute(v, "core", [(0, 1), (1, 0)])


def along_model(v, bit):
    return lax.ppermute(v, "model", [(i, i ^ bit) for i in range(X)])


def at(array, dz, dy, row=0, rows=ROWS, col=0, cols=None, base=0, half=0):
    return (array, dz, dy, row, rows, col, cols or array.shape[1], base, half)


def place(outs, blocks):
    arrays, copies = [], []
    for array, dz, dy, row, rows, col, cols, base, half in blocks:
        which = next((i for i, a in enumerate(arrays) if a is array), None)
        if which is None:
            which = len(arrays)
            arrays.append(array)
        while cols:
            out, start = divmod(base, W)
            width = min(cols, W - start)
            copies.append((which, row, rows, col, width, out, start, dz, dy, half))
            col, base, cols = col + width, base + width, cols - width
    n = len(arrays)

    def kernel(*refs):
        ins, (gate, up), sems = refs[:n], refs[-3:-1], refs[-1]
        z, y, c = (lax.axis_index(a) for a in SHARD)
        side = 2 * c - 1

        def moved(here, step, size):
            step = step[1] * side if isinstance(step, tuple) else step
            return lax.rem(here + step + size, size)

        started = []
        for i, (which, row, rows, col, width, out, start, dz, dy, half) in enumerate(copies):
            to = (moved(z, dz, Z) * Y + moved(y, dy, Y)) * ROWS
            if half:
                to = to + (c if half > 0 else 1 - c) * rows
            to = pl.multiple_of(to, 32)
            copy = pltpu.make_async_copy(
                ins[which].at[row : row + rows, col : col + width],
                (gate, up)[out].at[pl.ds(to, rows), start : start + width],
                sems.at[i],
            )
            copy.start()
            started.append(copy)
        for copy in started:
            copy.wait()

    either, hbm = (pl.BlockSpec(memory_space=m) for m in (pl.ANY, pltpu.HBM))
    shape = jax.ShapeDtypeStruct((Z * Y * ROWS, W), jnp.bfloat16)
    return pl.pallas_call(
        kernel,
        out_shape=(shape, shape),
        in_specs=[either] * n + [hbm] * len(outs),
        out_specs=(hbm, hbm),
        scratch_shapes=[pltpu.SemaphoreType.DMA((len(copies),))],
        input_output_aliases={n + i: i for i in range(len(outs))},
        compiler_params=pltpu.CompilerParams(vmem_limit_bytes=1 << 20),
    )(*arrays, *outs)


def local(one_gate, other_gate, one_up, other_up, mix_share, norm_train, norm_step):
    z, y, c = (lax.axis_index(a) for a in SHARD)
    x = lax.axis_index("model")
    first = c == 0
    low = -jnp.inf
    near, far = ("s", 1), ("s", -1)

    share = mix_share[:, None]
    mine = jnp.concatenate(
        [share * one_gate + (1.0 - share) * other_gate, share * one_up + (1.0 - share) * other_up],
        axis=1,
    )
    theirs = swap(mine)
    own = jnp.where(first, jnp.concatenate([mine, theirs]), jnp.concatenate([theirs, mine]))

    gain = lax.dynamic_update_slice(
        jnp.full((W,), low, jnp.float32), norm_train + norm_step, ((((z * Y + y) * C + c) * X + x) * 8,)
    )
    gain = jnp.maximum(gain, swap(gain))
    peak = jnp.concatenate([jnp.abs(own).max(0), gain])

    def halved(m):
        return jnp.concatenate([jnp.where(first, m[:W], m[W : 2 * W]), m[2 * W :]])

    def widened(h):
        return jnp.concatenate([jnp.where(first, h[:W], low), jnp.where(first, low, h[:W]), h[W:]])

    two, one = along_y(halved(peak), 2), along_y(peak)
    y1r = along_y(own)
    zBr = along_z(own[:, A:])
    peak = jnp.maximum(jnp.maximum(peak, one), widened(two))
    peak = jnp.maximum(peak, swap(peak))
    four = along_z(halved(peak), 4)
    sent = peak
    for k in (3, 2, 1):
        peak = jnp.maximum(peak, along_z(sent, k))
    peak = jnp.maximum(peak, widened(four))
    zAr = along_z(own[:, :A])
    zBxr = swap(zBr)
    y1xr = swap(y1r)
    y2r = along_y(jnp.where(first, y1r[:, :W], y1r[:, W:]))
    zAxr = swap(zAr)
    peak = jnp.maximum(peak, swap(peak))
    y2xr = swap(y2r)

    column = peak[None, : 2 * W]

    def narrow(v, base=0):
        return (v / column[:, base : base + v.shape[1]]).astype(jnp.bfloat16)

    def merged(v, w):
        return jnp.where(first, jnp.concatenate([v, w], axis=1), jnp.concatenate([w, v], axis=1))

    zB, zBx, zA, zAx = narrow(zBr, A), narrow(zBxr, A), narrow(zAr), narrow(zAxr)
    yr1 = along_y(jnp.concatenate([zB, zBx]))
    za2 = along_z(jnp.concatenate([zA, zB], axis=1))
    f0, f1, f1x, f2 = narrow(own), narrow(y1r), narrow(y1xr), narrow(merged(y2r, y2xr))
    zb1 = along_z(jnp.concatenate([f1[:, :A], f1x[:, :A], f2[:, :A]]))
    outs = place(
        (),
        [at(f0, 0, 0), at(f1, 0, near), at(f1x, 0, far), at(f2, 0, 2)]
        + [at(zA, near, 0), at(zAx, far, 0), at(zB, near, 0, base=A), at(zBx, far, 0, base=A)],
    )

    za3 = along_z(za2)
    za2x = swap(za2)
    yh1 = along_y(yr1[:ROWS])
    yr2 = along_y(jnp.concatenate([za2[:, A:], za2x[:, A:]]))
    zb2 = along_z(zb1)
    za4 = along_z(jnp.where(first, za3[:, :W], za3[:, W:]))
    za3x = swap(za3)
    yh2 = along_y(yr2[:ROWS])
    yr3 = along_y(jnp.concatenate([za3[:, A:], za3x[:, A:]]))
    y12 = jnp.concatenate([yr1, yh1, yr2, yh2])
    y12x = swap(y12)
    zb3 = along_z(zb2)
    z12 = jnp.concatenate([zb1, zb2])
    z12x = swap(z12)

    def from_z(v, k, end, row=0):
        d = ("s", k * end)
        return [
            at(v, d, ("s", end), row),
            at(v, d, ("s", -end), row + ROWS),
            at(v, d, 2, row + 2 * ROWS),
        ]

    def from_y(v, k, end, row=0):
        return [
            at(v, ("s", k * end), ("s", end), row, base=A),
            at(v, ("s", -k * end), ("s", end), row + ROWS, base=A),
        ]

    def from_y_half(v, k, end, row=0):
        return [at(v, ("s", k * end), 2, row, base=A)]

    outs = place(
        outs,
        [at(za2, ("s", 2), 0), at(za2x, ("s", -2), 0), at(za3, ("s", 3), 0), at(za3x, ("s", -3), 0)]
        + from_y(yr1, 1, 1) + from_y_half(yh1, 1, 1) + from_y(yr2, 2, 1) + from_y_half(yh2, 2, 1)
        + from_y(y12x, 1, -1) + from_y_half(y12x, 1, -1, 2 * ROWS)
        + from_y(y12x, 2, -1, 3 * ROWS) + from_y_half(y12x, 2, -1, 5 * ROWS),
    )
    za4x = swap(za4)
    f4 = merged(za4, za4x)
    yh3 = along_y(yr3[:ROWS])
    yr4 = along_y(f4[:, A:])
    half = ROWS // 2
    zb4 = along_z(
        jnp.concatenate([zb3[:ROWS], jnp.where(first, zb3[2 * ROWS : -half], zb3[-half:])])
    )
    outs = place(
        outs,
        [at(f4, 4, 0)] + from_z(zb1, 1, 1) + from_z(zb2, 2, 1)
        + from_z(z12x, 1, -1) + from_z(z12x, 2, -1, 3 * ROWS),
    )
    y34 = jnp.concatenate([yr3, yh3, yr4])
    y34x = swap(y34)
    zb3x = swap(zb3)
    yh4 = along_y(jnp.where(first, yr4[:half], yr4[half:]))
    gain = peak[2 * W :]
    gain = jnp.maximum(gain, along_model(gain, 1))
    outs = place(
        outs,
        from_y(yr3, 3, 1) + from_y_half(yh3, 3, 1) + [at(yr4, 4, near, base=A)]
        + from_y(y34x, 3, -1) + from_y_half(y34x, 3, -1, 2 * ROWS) + [at(y34x, 4, far, 3 * ROWS, base=A)]
        + from_z(zb3, 3, 1) + from_z(zb3x, 3, -1),
    )
    zb4x = swap(zb4)
    yh4x = swap(yh4)
    gain = jnp.maximum(gain, along_model(gain, 2))
    final_gate, final_up = place(
        outs,
        [at(zb4, 4, near), at(zb4, 4, 2, ROWS, half, half=1)]
        + [at(zb4x, 4, far), at(zb4x, 4, 2, ROWS, half, half=-1)]
        + [at(yh4, 4, 2, 0, half, base=A, half=1), at(yh4x, 4, 2, 0, half, base=A, half=-1)],
    )
    return final_gate, final_up, peak[:W], peak[W : 2 * W], gain.astype(jnp.bfloat16)


def solution(mesh):
    torus = Mesh(mesh.devices.reshape(Z, Y, C, X), ALL)
    return jax.shard_map(
        local,
        mesh=torus,
        in_specs=(P(SHARD, "model"),) * 4 + (P(SHARD), P(ALL), P(ALL)),
        out_specs=(P(None, "model"), P(None, "model"), P("model"), P("model"), P()),
        check_vma=False,
    )
```

time: 170 us -> 127 us (0.75)
  blocking collectives: 80.8 us -> 0 us
  starting transfers between devices: 0.04 us -> 73.6 us
  waiting for transfers between devices: 53 us -> 37.4 us
  local copies, waits for them, and re-layouts: 15.7 us -> 0.98 us
  between operations: 14.8 us -> 1.25 us
  Pallas kernels: 0 us -> 9.42 us
    ppermute x0 -> x44, starting transfers between devices: none -> 73.6 us  [the longest x17 29.5 us: swap(): return lax.ppermute(v, 'core', [(0, 1), (1, 0)])]
    all_gather x1 -> x0, waiting for transfers between devices: 53 us -> none  [side_by_side(): whole, at, outs = (lax.all_gather(both, axis, axis=dim, tiled=True), 0, [])]
    all_to_all x1 -> x0, blocking collectives: 41.1 us -> none  [copy_for_each(): return lax.all_to_all(copies, axis, split_axis=0, concat_axis=0, tiled=True)]
    ppermute x0 -> x44, waiting for transfers between devices: none -> 37.4 us  [the longest x13 18.4 us: along_z(): return lax.ppermute(v, SHARD, pairs(lambda z, y, c: (z + k * way(c), y, c)))]
    all_gather x3 -> x0, blocking collectives: 26.8 us -> none  [gather_in_order(): tiles = lax.all_gather(tiles, axes[k], axis=0, tiled=True)]
    unnamed x1 -> x0, blocking collectives: 12.8 us -> none
    slice x2 -> x19, local copies, waits for them, and re-layouts: 12 us -> 0.97 us  [the longest x1 0.6 us: local(): peak[W:2 * W]]
    pallas_call x0 -> x5, Pallas kernels: none -> 9.42 us  [place(): pl.pallas_call(kernel, out_shape=(shape, shape), in_specs=[either] * n +...]
  transfers between devices with their start and end apart: 1 -> 44, of which waited for: 1 -> 14; matrix products, arithmetic and copies ran while one was open for 2% -> 2% of each run, Pallas kernels for 0% -> 7%
where the time goes in v1:
time: 127 us
  starting transfers between devices  73.6 us (58%)
  waiting for transfers between devices  37.4 us (29%)
  Pallas kernels  9.42 us (7%)
  other arithmetic  4.26 us (3%)
    ppermute x17, starting transfers between devices, swap(): return lax.ppermute(v, 'core', [(0, 1), (1, 0)])  29.5 us
    ppermute x13, starting transfers between devices, along_z(): return lax.ppermute(v, SHARD, pairs(lambda z, y, c: (z + k * way(c), y, c)))  22.9 us
    ppermute x13, waiting for transfers between devices, along_z(): return lax.ppermute(v, SHARD, pairs(lambda z, y, c: (z + k * way(c), y, c)))  18.4 us
    ppermute x12, starting transfers between devices, along_y(): return lax.ppermute(v, SHARD, pairs(lambda z, y, c: (z, y + k * way(c), c)))  17.5 us
    ppermute x12, waiting for transfers between devices, along_y(): return lax.ppermute(v, SHARD, pairs(lambda z, y, c: (z, y + k * way(c), c)))  16.7 us
    pallas_call x5, Pallas kernels, place(): pl.pallas_call(kernel, out_shape=(shape, shape), in_specs=[either] * n +...  9.42 us
    ppermute x2, starting transfers between devices, along_model(): return lax.ppermute(v, 'model', [(i, i ^ bit) for i in range(X)])  3.66 us
  transfers between devices with their start and end apart: 44, of which 14 were waited for; matrix products, arithmetic and copies ran while one was open for 2% of the time, Pallas kernels for 7%

profile of v1, /device:TPU:1, one launch (start us, length us, event | category | flops | bytes accessed | tf_op | source)
XLA Modules:
  0.0 126.9 jit_solution(17654832750599464831)
XLA Ops:
  2.7 3.3 %collective-permute-start = (f32[32,4096]{1,0:T(8,128)S(1)}, f32[32,4096]{1,0:T(8,128)S(1)}, u32[]{:S(2)}, u32[]{:S(2)}) collective-permute-start(f32[32,4096]{1,0:T(8,128)S(1)} %pad_maximum_fusion.7), channel_id=1, source_target_pairs={{0,4},{4,0},{1,5},{5,1},{2,6},{6,2},{3,7},{7,3},{8,12},{12,8},{9,1... | collective-permute-start | bytes 1572872 | tf_op jit(solution)/shard_map/ppermute | solution.py:41
  12.0 2.7 %collective-permute-start.5 = (f32[6144]{0:T(1024)S(1)}, f32[6144]{0:T(1024)S(1)}, u32[]{:S(2)}, u32[]{:S(2)}) collective-permute-start(f32[6144]{0:T(1024)S(1)} %maximum_maximum_fusion), channel_id=1, source_target_pairs={{0,4},{4,0},{1,5},{5,1},{2,6},{6,2},{3,7},{7,3},{8,12},{12,8},{9,1... | collective-permute-start | bytes 73736 | tf_op jit(solution)/shard_map/ppermute | solution.py:41
  14.7 5.7 %collective-permute-start.19 = (f32[64,1536]{1,0:T(8,128)S(1)}, f32[64,1536]{1,0:T(8,128)S(1)}, u32[]{:S(2)}, u32[]{:S(2)}) collective-permute-start(f32[64,1536]{1,0:T(8,128)S(1)} %slice.170), channel_id=1, source_target_pairs={{0,32},{4,228},{8,40},{12,236},{16,48},{20,244},{24,56},{28,252},{... | collective-permute-start | bytes 1179656 | tf_op jit(solution)/shard_map/ppermute | solution.py:33
  22.8 3.6 %collective-permute-start.20 = (f32[64,2560]{1,0:T(8,128)S(1)}, f32[64,2560]{1,0:T(8,128)S(1)}, u32[]{:S(2)}, u32[]{:S(2)}) collective-permute-start(f32[64,2560]{1,0:T(8,128)S(1)} %slice.172), channel_id=1, source_target_pairs={{0,32},{4,228},{8,40},{12,236},{16,48},{20,244},{24,56},{28,252},{... | collective-permute-start | bytes 1966088 | tf_op jit(solution)/shard_map/ppermute | solution.py:33
  26.3 2.6 %collective-permute-done.9 = f32[4096]{0:T(1024)S(1)} collective-permute-done((f32[4096]{0:T(1024)S(1)}, f32[4096]{0:T(1024)S(1)}, u32[]{:S(2)}, u32[]{:S(2)}) %collective-permute-start.9) | collective-permute-done | bytes 16416 | tf_op jit(solution)/shard_map/ppermute | solution.py:33
  29.9 3.2 %collective-permute-start.41 = (f32[64,1536]{1,0:T(8,128)S(1)}, f32[64,1536]{1,0:T(8,128)S(1)}, u32[]{:S(2)}, u32[]{:S(2)}) collective-permute-start(f32[64,1536]{1,0:T(8,128)S(1)} %collective-permute-done.19), channel_id=1, source_target_pairs={{0,4},{4,0},{1,5},{5,1},{2,6},{6,2},{3,7},{7,3},{8,12},{12,8},{9,1... | collective-permute-start | bytes 1179656 | tf_op jit(solution)/shard_map/ppermute | solution.py:41
  34.7 3.5 %collective-permute-start.10 = (f32[6144]{0:T(1024)S(1)}, f32[6144]{0:T(1024)S(1)}, u32[]{:S(2)}, u32[]{:S(2)}) collective-permute-start(f32[6144]{0:T(1024)S(1)} %maximum_maximum_fusion.1), channel_id=1, source_target_pairs={{0,4},{4,0},{1,5},{5,1},{2,6},{6,2},{3,7},{7,3},{8,12},{12,8},{9,1... | collective-permute-start | bytes 73736 | tf_op jit(solution)/shard_map/ppermute | solution.py:41
  39.7 2.8 %collective-permute-start.12 = (f32[64,2048]{1,0:T(8,128)S(1)}, f32[64,2048]{1,0:T(8,128)S(1)}, u32[]{:S(2)}, u32[]{:S(2)}) collective-permute-start(f32[64,2048]{1,0:T(8,128)S(1)} %slice_select_fusion), channel_id=1, source_target_pairs={{0,8},{4,28},{8,16},{12,4},{16,24},{20,12},{24,0},{28,20},{32,40},... | collective-permute-start | bytes 1572872 | tf_op jit(solution)/shard_map/ppermute | solution.py:37
  43.8 4.8 %collective-permute-done.12 = f32[64,2048]{1,0:T(8,128)S(1)} collective-permute-done((f32[64,2048]{1,0:T(8,128)S(1)}, f32[64,2048]{1,0:T(8,128)S(1)}, u32[]{:S(2)}, u32[]{:S(2)}) %collective-permute-start.12) | collective-permute-done | bytes 524320 | tf_op jit(solution)/shard_map/ppermute | solution.py:37
  48.6 3.2 %collective-permute-start.13 = (f32[64,2048]{1,0:T(8,128)S(1)}, f32[64,2048]{1,0:T(8,128)S(1)}, u32[]{:S(2)}, u32[]{:S(2)}) collective-permute-start(f32[64,2048]{1,0:T(8,128)S(1)} %collective-permute-done.12), channel_id=1, source_target_pairs={{0,4},{4,0},{1,5},{5,1},{2,6},{6,2},{3,7},{7,3},{8,12},{12,8},{9,1... | collective-permute-start | bytes 1572872 | tf_op jit(solution)/shard_map/ppermute | solution.py:41
  57.0 2.9 %collective-permute-start.38 = (bf16[128,2560]{1,0:T(8,128)(2,1)S(1)}, bf16[128,2560]{1,0:T(8,128)(2,1)S(1)}, u32[]{:S(2)}, u32[]{:S(2)}) collective-permute-start(bf16[128,2560]{1,0:T(8,128)(2,1)S(1)} %pad_maximum_fusion.5), channel_id=1, source_target_pairs={{0,8},{4,28},{8,16},{12,4},{16,24},{20,12},{24,0},{28,20},{32,40},... | collective-permute-start | bytes 1966088 | tf_op jit(solution)/shard_map/ppermute | solution.py:37
  59.9 2.3 %collective-permute-done.22.refs_2_ = bf16[64,4096]{1,0:T(8,128)(2,1)S(1)} collective-permute-done((bf16[64,4096]{1,0:T(8,128)(2,1)S(1)}, bf16[64,4096]{1,0:T(8,128)(2,1)S(1)}, u32[]{:S(2)}, u32[]{:S(2)}) %collective-permute-start.22) | collective-permute-done | bytes 524320 | tf_op jit(solution)/shard_map/ppermute | solution.py:33
  65.2 2.5 %collective-permute-start.43 = (bf16[2048]{0:T(1024)(128)(2,1)S(1)}, bf16[2048]{0:T(1024)(128)(2,1)S(1)}, u32[]{:S(2)}, u32[]{:S(2)}) collective-permute-start(bf16[2048]{0:T(1024)(128)(2,1)S(1)} %slice_maximum_fusion), channel_id=1, source_target_pairs={{0,2},{1,3},{2,0},{3,1},{4,6},{5,7},{6,4},{7,5},{8,10},{9,11},{10,... | collective-permute-start | bytes 12296 | tf_op jit(solution)/shard_map/ppermute | solution.py:45
  67.7 3.6 %collective-permute-done.23 = bf16[64,2048]{1,0:T(8,128)(2,1)S(1)} collective-permute-done((bf16[64,2048]{1,0:T(8,128)(2,1)S(1)}, bf16[64,2048]{1,0:T(8,128)(2,1)S(1)}, u32[]{:S(2)}, u32[]{:S(2)}) %collective-permute-start.23) | collective-permute-done | bytes 262176 | tf_op jit(solution)/shard_map/ppermute | solution.py:33
  71.3 2.6 %collective-permute-start.37 = (bf16[64,2560]{1,0:T(8,128)(2,1)S(1)}, bf16[64,2560]{1,0:T(8,128)(2,1)S(1)}, u32[]{:S(2)}, u32[]{:S(2)}) collective-permute-start(bf16[64,2560]{1,0:T(8,128)(2,1)S(1)} %slice.182), channel_id=1, source_target_pairs={{0,8},{4,28},{8,16},{12,4},{16,24},{20,12},{24,0},{28,20},{32,40},... | collective-permute-start | bytes 983048 | tf_op jit(solution)/shard_map/ppermute | solution.py:37
  78.9 2.4 %collective-permute-start.25 = (bf16[64,2560]{1,0:T(8,128)(2,1)S(1)}, bf16[64,2560]{1,0:T(8,128)(2,1)S(1)}, u32[]{:S(2)}, u32[]{:S(2)}) collective-permute-start(bf16[64,2560]{1,0:T(8,128)(2,1)S(1)} %slice.176), channel_id=1, source_target_pairs={{0,8},{4,28},{8,16},{12,4},{16,24},{20,12},{24,0},{28,20},{32,40},... | collective-permute-start | bytes 983048 | tf_op jit(solution)/shard_map/ppermute | solution.py:37
  81.3 8.9 %collective-permute-done.39.refs_7_ = bf16[64,2560]{1,0:T(8,128)(2,1)S(1)} collective-permute-done((bf16[64,2560]{1,0:T(8,128)(2,1)S(1)}, bf16[64,2560]{1,0:T(8,128)(2,1)S(1)}, u32[]{:S(2)}, u32[]{:S(2)}) %collective-permute-start.39) | collective-permute-done | bytes 327712 | tf_op jit(solution)/shard_map/ppermute | solution.py:37
  95.2 2.9 %collective-permute-start.16 = (bf16[192,1536]{1,0:T(8,128)(2,1)S(1)}, bf16[192,1536]{1,0:T(8,128)(2,1)S(1)}, u32[]{:S(2)}, u32[]{:S(2)}) collective-permute-start(bf16[192,1536]{1,0:T(8,128)(2,1)S(1)} %collective-permute-done.15.refs_2_), channel_id=1, source_target_pairs={{0,32},{4,228},{8,40},{12,236},{16,48},{20,244},{24,56},{28,252},{... | collective-permute-start | bytes 1769480 | tf_op jit(solution)/shard_map/ppermute | solution.py:33
  98.9 2.2 %collective-permute-start.31 = (bf16[256,2560]{1,0:T(8,128)(2,1)S(1)}, bf16[256,2560]{1,0:T(8,128)(2,1)S(1)}, u32[]{:S(2)}, u32[]{:S(2)}) collective-permute-start(bf16[256,2560]{1,0:T(8,128)(2,1)S(1)} %pad_maximum_fusion.1), channel_id=1, source_target_pairs={{0,4},{4,0},{1,5},{5,1},{2,6},{6,2},{3,7},{7,3},{8,12},{12,8},{9,1... | collective-permute-start | bytes 3932168 | tf_op jit(solution)/shard_map/ppermute | solution.py:41
  101.2 3.7 %collective-permute-done.16.refs_4_ = bf16[192,1536]{1,0:T(8,128)(2,1)S(1)} collective-permute-done((bf16[192,1536]{1,0:T(8,128)(2,1)S(1)}, bf16[192,1536]{1,0:T(8,128)(2,1)S(1)}, u32[]{:S(2)}, u32[]{:S(2)}) %collective-permute-start.16) | collective-permute-done | bytes 589856 | tf_op jit(solution)/shard_map/ppermute | solution.py:33
  104.9 2.4 %collective-permute-start.33 = (bf16[384,1536]{1,0:T(8,128)(2,1)S(1)}, bf16[384,1536]{1,0:T(8,128)(2,1)S(1)}, u32[]{:S(2)}, u32[]{:S(2)}) collective-permute-start(bf16[384,1536]{1,0:T(8,128)(2,1)S(1)} %pad_maximum_fusion.2), channel_id=1, source_target_pairs={{0,4},{4,0},{1,5},{5,1},{2,6},{6,2},{3,7},{7,3},{8,12},{12,8},{9,1... | collective-permute-start | bytes 3538952 | tf_op jit(solution)/shard_map/ppermute | solution.py:41
  108.7 4.7 %collective-permute-done.17.refs_0_ = bf16[96,1536]{1,0:T(8,128)(2,1)S(1)} collective-permute-done((bf16[96,1536]{1,0:T(8,128)(2,1)S(1)}, bf16[96,1536]{1,0:T(8,128)(2,1)S(1)}, u32[]{:S(2)}, u32[]{:S(2)}) %collective-permute-start.17) | collective-permute-done | bytes 294944 | tf_op jit(solution)/shard_map/ppermute | solution.py:33
  113.4 2.6 %collective-permute-start.18 = (bf16[96,1536]{1,0:T(8,128)(2,1)S(1)}, bf16[96,1536]{1,0:T(8,128)(2,1)S(1)}, u32[]{:S(2)}, u32[]{:S(2)}) collective-permute-start(bf16[96,1536]{1,0:T(8,128)(2,1)S(1)} %collective-permute-done.17.refs_0_), channel_id=1, source_target_pairs={{0,4},{4,0},{1,5},{5,1},{2,6},{6,2},{3,7},{7,3},{8,12},{12,8},{9,1... | collective-permute-start | bytes 884744 | tf_op jit(solution)/shard_map/ppermute | solution.py:41
  119.0 2.9 %shard_map.111 = (bf16[2048,2048]{1,0:T(8,128)(2,1)}, bf16[2048,2048]{1,0:T(8,128)(2,1)}) custom-call(bf16[64,4096]{1,0:T(8,128)(2,1)S(1)} %collective-permute-done.21.refs_0_, bf16[64,4096]{1,0:T(8,128)(2,1)S(1)} %collective-permute-done.34.refs_1_, ...), custom_call_target="tpu_custom_call", output_to_operand_aliasing={{0}: (9, {}), {1}: (10, {})} | custom-call | tf_op jit(solution)/shard_map/pallas_call | solution.py:93
  (129 shorter events, 44.0 us)
Async XLA Ops:
  14.7 15.2 %collective-permute-start.19 = (f32[64,1536]{1,0:T(8,128)S(1)}, f32[64,1536]{1,0:T(8,128)S(1)}, u32[]{:S(2)}, u32[]{:S(2)}) collective-permute-start(f32[64,1536]{1,0:T(8,128)S(1)} %slice.170), channel_id=1, source_target_pairs={{0,32},{4,228},{8,40},{12,236},{16,48},{20,244},{24,56},{28,252},{... | collective-permute-start | bytes 1179656 | tf_op jit(solution)/shard_map/ppermute | solution.py:33
  22.7 16.9 %collective-permute-start.1 = (f32[64,4096]{1,0:T(8,128)S(1)}, f32[64,4096]{1,0:T(8,128)S(1)}, u32[]{:S(2)}, u32[]{:S(2)}) collective-permute-start(f32[64,4096]{1,0:T(8,128)S(1)} %get-tuple-element.26), channel_id=1, source_target_pairs={{0,8},{4,28},{8,16},{12,4},{16,24},{20,12},{24,0},{28,20},{32,40},... | collective-permute-start | bytes 3145736 | tf_op jit(solution)/shard_map/ppermute | solution.py:37
  22.8 16.3 %collective-permute-start.20 = (f32[64,2560]{1,0:T(8,128)S(1)}, f32[64,2560]{1,0:T(8,128)S(1)}, u32[]{:S(2)}, u32[]{:S(2)}) collective-permute-start(f32[64,2560]{1,0:T(8,128)S(1)} %slice.172), channel_id=1, source_target_pairs={{0,32},{4,228},{8,40},{12,236},{16,48},{20,244},{24,56},{28,252},{... | collective-permute-start | bytes 1966088 | tf_op jit(solution)/shard_map/ppermute | solution.py:33
  29.9 9.6 %collective-permute-start.41 = (f32[64,1536]{1,0:T(8,128)S(1)}, f32[64,1536]{1,0:T(8,128)S(1)}, u32[]{:S(2)}, u32[]{:S(2)}) collective-permute-start(f32[64,1536]{1,0:T(8,128)S(1)} %collective-permute-done.19), channel_id=1, source_target_pairs={{0,4},{4,0},{1,5},{5,1},{2,6},{6,2},{3,7},{7,3},{8,12},{12,8},{9,1... | collective-permute-start | bytes 1179656 | tf_op jit(solution)/shard_map/ppermute | solution.py:41
  42.5 13.1 %collective-permute-start.11 = (f32[64,4096]{1,0:T(8,128)S(1)}, f32[64,4096]{1,0:T(8,128)S(1)}, u32[]{:S(2)}, u32[]{:S(2)}) collective-permute-start(f32[64,4096]{1,0:T(8,128)S(1)} %collective-permute-done.1), channel_id=1, source_target_pairs={{0,4},{4,0},{1,5},{5,1},{2,6},{6,2},{3,7},{7,3},{8,12},{12,8},{9,1... | collective-permute-start | bytes 3145736 | tf_op jit(solution)/shard_map/ppermute | solution.py:41
  42.6 10.7 %collective-permute-start.21 = (bf16[64,4096]{1,0:T(8,128)(2,1)S(1)}, bf16[64,4096]{1,0:T(8,128)(2,1)S(1)}, u32[]{:S(2)}, u32[]{:S(2)}) collective-permute-start(bf16[64,4096]{1,0:T(8,128)(2,1)S(1)} %pad_maximum_fusion.8), channel_id=1, source_target_pairs={{0,32},{4,228},{8,40},{12,236},{16,48},{20,244},{24,56},{28,252},{... | collective-permute-start | bytes 1572872 | tf_op jit(solution)/shard_map/ppermute | solution.py:33
  51.7 12.6 %collective-permute-start.42 = (bf16[2048]{0:T(1024)(128)(2,1)S(1)}, bf16[2048]{0:T(1024)(128)(2,1)S(1)}, u32[]{:S(2)}, u32[]{:S(2)}) collective-permute-start(bf16[2048]{0:T(1024)(128)(2,1)S(1)} %slice.188), channel_id=1, source_target_pairs={{0,1},{1,0},{2,3},{3,2},{4,5},{5,4},{6,7},{7,6},{8,9},{9,8},{10,11... | collective-permute-start | bytes 12296 | tf_op jit(solution)/shard_map/ppermute | solution.py:45
  53.0 12.2 %collective-permute-start.36 = (bf16[128,2560]{1,0:T(8,128)(2,1)S(1)}, bf16[128,2560]{1,0:T(8,128)(2,1)S(1)}, u32[]{:S(2)}, u32[]{:S(2)}) collective-permute-start(bf16[128,2560]{1,0:T(8,128)(2,1)S(1)} %pad_maximum_fusion.4), channel_id=1, source_target_pairs={{0,8},{4,28},{8,16},{12,4},{16,24},{20,12},{24,0},{28,20},{32,40},... | collective-permute-start | bytes 1966088 | tf_op jit(solution)/shard_map/ppermute | solution.py:37
  56.1 17.8 %collective-permute-start.14 = (bf16[192,1536]{1,0:T(8,128)(2,1)S(1)}, bf16[192,1536]{1,0:T(8,128)(2,1)S(1)}, u32[]{:S(2)}, u32[]{:S(2)}) collective-permute-start(bf16[192,1536]{1,0:T(8,128)(2,1)S(1)} %pad_maximum_fusion.6), channel_id=1, source_target_pairs={{0,32},{4,228},{8,40},{12,236},{16,48},{20,244},{24,56},{28,252},{... | collective-permute-start | bytes 1769480 | tf_op jit(solution)/shard_map/ppermute | solution.py:33
  57.0 19.9 %collective-permute-start.38 = (bf16[128,2560]{1,0:T(8,128)(2,1)S(1)}, bf16[128,2560]{1,0:T(8,128)(2,1)S(1)}, u32[]{:S(2)}, u32[]{:S(2)}) collective-permute-start(bf16[128,2560]{1,0:T(8,128)(2,1)S(1)} %pad_maximum_fusion.5), channel_id=1, source_target_pairs={{0,8},{4,28},{8,16},{12,4},{16,24},{20,12},{24,0},{28,20},{32,40},... | collective-permute-start | bytes 1966088 | tf_op jit(solution)/shard_map/ppermute | solution.py:37
  62.2 12.8 %collective-permute-start.28 = (bf16[64,4096]{1,0:T(8,128)(2,1)S(1)}, bf16[64,4096]{1,0:T(8,128)(2,1)S(1)}, u32[]{:S(2)}, u32[]{:S(2)}) collective-permute-start(bf16[64,4096]{1,0:T(8,128)(2,1)S(1)} %collective-permute-done.22.refs_2_), channel_id=1, source_target_pairs={{0,4},{4,0},{1,5},{5,1},{2,6},{6,2},{3,7},{7,3},{8,12},{12,8},{9,1... | collective-permute-start | bytes 1572872 | tf_op jit(solution)/shard_map/ppermute | solution.py:41
  65.2 42.1 %collective-permute-start.43 = (bf16[2048]{0:T(1024)(128)(2,1)S(1)}, bf16[2048]{0:T(1024)(128)(2,1)S(1)}, u32[]{:S(2)}, u32[]{:S(2)}) collective-permute-start(bf16[2048]{0:T(1024)(128)(2,1)S(1)} %slice_maximum_fusion), channel_id=1, source_target_pairs={{0,2},{1,3},{2,0},{3,1},{4,6},{5,7},{6,4},{7,5},{8,10},{9,11},{10,... | collective-permute-start | bytes 12296 | tf_op jit(solution)/shard_map/ppermute | solution.py:45
  75.0 20.2 %collective-permute-start.15 = (bf16[192,1536]{1,0:T(8,128)(2,1)S(1)}, bf16[192,1536]{1,0:T(8,128)(2,1)S(1)}, u32[]{:S(2)}, u32[]{:S(2)}) collective-permute-start(bf16[192,1536]{1,0:T(8,128)(2,1)S(1)} %collective-permute-done.14.refs_1_), channel_id=1, source_target_pairs={{0,32},{4,228},{8,40},{12,236},{16,48},{20,244},{24,56},{28,252},{... | collective-permute-start | bytes 1769480 | tf_op jit(solution)/shard_map/ppermute | solution.py:33
  76.9 15.6 %collective-permute-start.29 = (bf16[128,2560]{1,0:T(8,128)(2,1)S(1)}, bf16[128,2560]{1,0:T(8,128)(2,1)S(1)}, u32[]{:S(2)}, u32[]{:S(2)}) collective-permute-start(bf16[128,2560]{1,0:T(8,128)(2,1)S(1)} %pad_maximum_fusion.3), channel_id=1, source_target_pairs={{0,8},{4,28},{8,16},{12,4},{16,24},{20,12},{24,0},{28,20},{32,40},... | collective-permute-start | bytes 1966088 | tf_op jit(solution)/shard_map/ppermute | solution.py:37
  77.2 13.0 %collective-permute-start.39 = (bf16[64,2560]{1,0:T(8,128)(2,1)S(1)}, bf16[64,2560]{1,0:T(8,128)(2,1)S(1)}, u32[]{:S(2)}, u32[]{:S(2)}) collective-permute-start(bf16[64,2560]{1,0:T(8,128)(2,1)S(1)} %slice.185), channel_id=1, source_target_pairs={{0,8},{4,28},{8,16},{12,4},{16,24},{20,12},{24,0},{28,20},{32,40},... | collective-permute-start | bytes 983048 | tf_op jit(solution)/shard_map/ppermute | solution.py:37
  78.9 15.0 %collective-permute-start.25 = (bf16[64,2560]{1,0:T(8,128)(2,1)S(1)}, bf16[64,2560]{1,0:T(8,128)(2,1)S(1)}, u32[]{:S(2)}, u32[]{:S(2)}) collective-permute-start(bf16[64,2560]{1,0:T(8,128)(2,1)S(1)} %slice.176), channel_id=1, source_target_pairs={{0,8},{4,28},{8,16},{12,4},{16,24},{20,12},{24,0},{28,20},{32,40},... | collective-permute-start | bytes 983048 | tf_op jit(solution)/shard_map/ppermute | solution.py:37
  90.4 25.6 %collective-permute-start.40 = (bf16[384,2560]{1,0:T(8,128)(2,1)S(1)}, bf16[384,2560]{1,0:T(8,128)(2,1)S(1)}, u32[]{:S(2)}, u32[]{:S(2)}) collective-permute-start(bf16[384,2560]{1,0:T(8,128)(2,1)S(1)} %pad_maximum_fusion), channel_id=1, source_target_pairs={{0,4},{4,0},{1,5},{5,1},{2,6},{6,2},{3,7},{7,3},{8,12},{12,8},{9,1... | collective-permute-start | bytes 5898248 | tf_op jit(solution)/shard_map/ppermute | solution.py:41
  93.9 13.6 %collective-permute-start.26 = (bf16[32,2560]{1,0:T(8,128)(2,1)S(1)}, bf16[32,2560]{1,0:T(8,128)(2,1)S(1)}, u32[]{:S(2)}, u32[]{:S(2)}) collective-permute-start(bf16[32,2560]{1,0:T(8,128)(2,1)S(1)} %slice_select_fusion.2), channel_id=1, source_target_pairs={{0,8},{4,28},{8,16},{12,4},{16,24},{20,12},{24,0},{28,20},{32,40},... | collective-permute-start | bytes 491528 | tf_op jit(solution)/shard_map/ppermute | solution.py:37
  95.2 9.7 %collective-permute-start.16 = (bf16[192,1536]{1,0:T(8,128)(2,1)S(1)}, bf16[192,1536]{1,0:T(8,128)(2,1)S(1)}, u32[]{:S(2)}, u32[]{:S(2)}) collective-permute-start(bf16[192,1536]{1,0:T(8,128)(2,1)S(1)} %collective-permute-done.15.refs_2_), channel_id=1, source_target_pairs={{0,32},{4,228},{8,40},{12,236},{16,48},{20,244},{24,56},{28,252},{... | collective-permute-start | bytes 1769480 | tf_op jit(solution)/shard_map/ppermute | solution.py:33
  98.9 24.6 %collective-permute-start.31 = (bf16[256,2560]{1,0:T(8,128)(2,1)S(1)}, bf16[256,2560]{1,0:T(8,128)(2,1)S(1)}, u32[]{:S(2)}, u32[]{:S(2)}) collective-permute-start(bf16[256,2560]{1,0:T(8,128)(2,1)S(1)} %pad_maximum_fusion.1), channel_id=1, source_target_pairs={{0,4},{4,0},{1,5},{5,1},{2,6},{6,2},{3,7},{7,3},{8,12},{12,8},{9,1... | collective-permute-start | bytes 3932168 | tf_op jit(solution)/shard_map/ppermute | solution.py:41
  104.9 17.0 %collective-permute-start.33 = (bf16[384,1536]{1,0:T(8,128)(2,1)S(1)}, bf16[384,1536]{1,0:T(8,128)(2,1)S(1)}, u32[]{:S(2)}, u32[]{:S(2)}) collective-permute-start(bf16[384,1536]{1,0:T(8,128)(2,1)S(1)} %pad_maximum_fusion.2), channel_id=1, source_target_pairs={{0,4},{4,0},{1,5},{5,1},{2,6},{6,2},{3,7},{7,3},{8,12},{12,8},{9,1... | collective-permute-start | bytes 3538952 | tf_op jit(solution)/shard_map/ppermute | solution.py:41
  107.3 16.2 %collective-permute-start.32 = (bf16[192,1536]{1,0:T(8,128)(2,1)S(1)}, bf16[192,1536]{1,0:T(8,128)(2,1)S(1)}, u32[]{:S(2)}, u32[]{:S(2)}) collective-permute-start(bf16[192,1536]{1,0:T(8,128)(2,1)S(1)} %collective-permute-done.16.refs_4_), channel_id=1, source_target_pairs={{0,4},{4,0},{1,5},{5,1},{2,6},{6,2},{3,7},{7,3},{8,12},{12,8},{9,1... | collective-permute-start | bytes 1769480 | tf_op jit(solution)/shard_map/ppermute | solution.py:41
  113.4 12.3 %collective-permute-start.18 = (bf16[96,1536]{1,0:T(8,128)(2,1)S(1)}, bf16[96,1536]{1,0:T(8,128)(2,1)S(1)}, u32[]{:S(2)}, u32[]{:S(2)}) collective-permute-start(bf16[96,1536]{1,0:T(8,128)(2,1)S(1)} %collective-permute-done.17.refs_0_), channel_id=1, source_target_pairs={{0,4},{4,0},{1,5},{5,1},{2,6},{6,2},{3,7},{7,3},{8,12},{12,8},{9,1... | collective-permute-start | bytes 884744 | tf_op jit(solution)/shard_map/ppermute | solution.py:41
  116.0 9.7 %collective-permute-start.27 = (bf16[32,2560]{1,0:T(8,128)(2,1)S(1)}, bf16[32,2560]{1,0:T(8,128)(2,1)S(1)}, u32[]{:S(2)}, u32[]{:S(2)}) collective-permute-start(bf16[32,2560]{1,0:T(8,128)(2,1)S(1)} %collective-permute-done.26.refs_2_), channel_id=1, source_target_pairs={{0,4},{4,0},{1,5},{5,1},{2,6},{6,2},{3,7},{7,3},{8,12},{12,8},{9,1... | collective-permute-start | bytes 491528 | tf_op jit(solution)/shard_map/ppermute | solution.py:41
  (22 other events, 123.0 us)
